TPU v7x, 128 devices: a whole 4x4x4 slice. The times are simulated.
128 devices in a mesh: stn: 32 (over z_hi, y, x), pts: 2 (over core), freq: 2 (over z_lo).
Axes of the slice: x: 4, y: 4, z: 4 (z_hi: 2, z_lo: 2; z = z_hi * 2 + z_lo), core: 2. Of those that a mesh axis runs over, the one named last changes fastest.
Arguments:
- greens: bfloat16 [2, 4, 2048, 4096], P(None, 'freq', 'stn', 'pts'), may hold values from -6 to 6
- noise_weights: bfloat16 [2, 4, 2048, 2048], P(None, 'freq', 'stn'), may hold values from -12 to 12, as said below
Outputs:
- kernel: float32 [4096], P('pts')
Inputs may be any that keep to these rules, and one draw needn't show every extreme that they name: For every frequency, noise_weights[0] is symmetric and noise_weights[1] antisymmetric in the two station dimensions, so each frequency's matrix is Hermitian.
All inputs are finite; a program needn't handle non-finite values. Where the computation divides by a largest or mean magnitude, that divisor is 1e-20 or more.
Results may differ from a plain program's by a relative error of at most 0.0003.
Values may be sent and summed in bfloat16 or wider, within the bound.
A program may use at most 192 MiB of HBM per device.

v0:
```python
import jax
import jax.numpy as jnp
from jax import lax
from jax.sharding import PartitionSpec as P


def from_everyone(x, axis):
    size = lax.axis_size(axis)
    return lax.all_to_all(jnp.broadcast_to(x[None], (size, *x.shape)), axis, 0, 0, tiled=True)


def of_everyone(x, axis):
    everything = from_everyone(x, axis)
    return jnp.sum(everything, axis=0)


def taken_together(x, axis):
    return from_everyone(x, axis).max(axis=0)


def mixing_of(weights):
    negated = -weights[1]
    return jnp.stack([jnp.stack([weights[0], negated]), jnp.stack([weights[1], weights[0]])])


def body(greens, noise_weights):
    stations = noise_weights.shape[3]
    mixing = mixing_of(noise_weights)
    summed = jnp.einsum(
        "ocfin,cfnx->ofix",
        mixing,
        lax.all_gather(greens, "stn", axis=2, tiled=True),
        preferred_element_type=jnp.float32,
    )
    green_real = greens[0].astype(jnp.float32)
    green_imag = greens[1].astype(jnp.float32)
    partial_kernel = (
        jnp.sum(green_real * summed[0] + green_imag * summed[1], axis=(0, 1)) / stations
    )
    raw_kernel = of_everyone(partial_kernel, ("stn", "freq"))
    largest = taken_together(jnp.max(jnp.abs(raw_kernel)), "pts")
    return raw_kernel / (largest + 1e-06)


def solution(mesh):
    in_specs = (P(None, "freq", "stn", "pts"), P(None, "freq", "stn", None))
    out_specs = P("pts")
    return jax.shard_map(body, mesh=mesh, in_specs=in_specs, out_specs=out_specs, check_vma=False)
```

profile of v0, /device:TPU:1, one launch (start us, length us, event | category | flops | bytes accessed | tf_op | source)
XLA Modules:
  0.0 321.7 jit_solution(8327975592831360117)
XLA Ops:
  6.5 0.0 copy-start.1
  6.5 0.0 all-gather.2.cloned.1.call-start
  6.5 2.4 copy.15
  8.9 0.0 all-gather.2.cloned.1.call-update
  9.0 0.0 copy-done.1
  9.0 0.1 slice_bitcast_fusion
  9.1 0.2 maximum_bitcast_fusion
  9.3 265.1 %all-gather.2.cloned.1.call-done = bf16[2,2,2048,2048]{3,2,0,1:T(8,128)(2,1)} async-done(((bf16[2,2,64,2048]{3,2,0,1:T(8,128)(2,1)}), bf16[2,2,2048,2048]{3,2,0,1:T(8,128)(2,1)}) %all-gather.2.cloned.1.call-update) | async-done | bytes 33554448 | tf_op jit(solution)/shard_map/all_gather | solution.py:32
  274.4 0.0 copy-start
  274.4 13.0 %fusion.2 = f32[2,2,64,2048]{3,2,0,1:T(8,128)S(1)} fusion(bf16[2,2,2048,2048]{3,2,0,1:T(8,128)(2,1)} %all-gather.2.cloned.1.call-done, bf16[1,2,2,64,2048]{4,3,1,0,2:T(8,128)(2,1)S(1)} %get-tuple-element.8, bf16[1,2,2,64,2048]{4,3,1,0,2:T(8,128)(2,1)S(1)} %get-tuple-element.7), kind=kOutput, calls=%fused_computation.2 | convolution fusion | flops 4296015872 | bytes 37748736 | tf_op jit(solution)/shard_map/ocfin,cfnx->ofix/dot_general | solution.py:29
  287.4 0.0 copy-done
  287.4 0.3 fusion.9
  287.7 0.3 broadcast_in_dim.4
  287.9 16.9 %all_to_all.12 = f32[64,1,2048]{2,1,0:T(1,128)S(1)} all-to-all(f32[64,1,2048]{2,1,0:T(1,128)S(1)} %broadcast_in_dim.4), channel_id=1, replica_groups=mesh['stn'=32,'pts'=2,'freq'=2] {'stn','freq'}, dimensions={0} | all-to-all | bytes 1048576 | tf_op jit(solution)/shard_map/all_to_all | solution.py:9
  304.9 0.3 reduce_sum.19
  305.2 0.6 abs_reduce_fusion
  305.8 0.6 broadcast_in_dim.5
  306.5 6.5 %all_to_all.13 = f32[2,1,1]{2,1,0:T(1,128)S(1)} all-to-all(f32[2,1,1]{2,1,0:T(1,128)S(1)} %broadcast_in_dim.5), channel_id=1, replica_groups=mesh['stn'=32,'pts'=2,'freq'=2] {'pts'}, dimensions={0} | all-to-all | bytes 16 | tf_op jit(solution)/shard_map/all_to_all | solution.py:9
  313.0 0.6 reduce_max.19
  314.2 0.6 broadcast_divide_fusion
  (2 shorter events, 0.0 us)
Async XLA Ops:
  6.5 2.4 copy-start.1
  6.5 267.8 %all-gather.2.cloned.1.call-start = ((), (), s32[]{:S(2)}) async-start(), calls=%async_computation.2 | async-start | bytes 34603008 | tf_op jit(solution)/shard_map/all_gather | solution.py:32
  274.4 13.0 %copy-start = (bf16[2,2,64,2048]{3,2,1,0:T(8,128)(2,1)S(1)}, bf16[2,2,64,2048]{3,2,1,0:T(8,128)(2,1)}, u32[]{:S(2)}) copy-start(bf16[2,2,64,2048]{3,2,1,0:T(8,128)(2,1)} %param.2) | copy-start | bytes 3145732
Sparse Core Ops, SparseCore 0:
  10.5 263.8 all-gather.1
where the time goes:
time: 322 us
  waiting for transfers between devices  265 us (82%)
  blocking collectives  23.5 us (7%)
  between operations  14.1 us (4%)
  matrix products  13 us (4%)
  local copies, waits for them, and re-layouts  3.4 us (1%)
    all_gather x1, waiting for transfers between devices, body(): lax.all_gather(greens, 'stn', axis=2, tiled=True)  265 us
    all_to_all x2, blocking collectives, from_everyone(): lax.all_to_all(jnp.broadcast_to(x[None], (size, *x.shape)), axis, 0, 0, t...  23.5 us
    dot_general x1, matrix products, body(): jnp.einsum('ocfin,cfnx->ofix', mixing, lax.all_gather(greens, 'stn', axis...  13 us
  transfers between devices with their start and end apart: 1, of which 1 were waited for; matrix products, arithmetic and copies ran while one was open for 0% of the time, Pallas kernels for 0%

commit v1 on v0

v1 whole, which is shorter than its diff:
```python
import jax
import jax.numpy as jnp
from jax import lax
from jax.experimental import pallas as pl
from jax.experimental.pallas import tpu as pltpu
from jax.sharding import PartitionSpec as P

MESH = pl.DeviceIdType.MESH
SIDE = 4
RUN = 64
BLOCK = 512
POINTS = 512
HALF = 256

SPREAD = [(dx, 0, dz, 0) for dx in (0, 1, 3, 2) for dz in (1, 3)]
PLANE = [(0, dy, dz, 0) for dz in range(SIDE) for dy in range(SIDE) if dy or dz]
ROW = [(dx, 0, 0, dc) for dx in range(SIDE) for dc in range(2) if dx or dc]
PARTNERS = list(dict.fromkeys(SPREAD + PLANE + ROW))


def place():
    stn = lax.axis_index("stn")
    x, y = stn % SIDE, stn // SIDE % SIDE
    z = stn // (SIDE * SIDE) * 2 + lax.axis_index("freq")
    return x, y, z, lax.axis_index("pts")


def device(here, dx=0, dy=0, dz=0, dc=0):
    x, y, z, core = here
    x, y, z, core = (x + dx) % SIDE, (y + dy) % SIDE, (z + dz) % SIDE, (core + dc) % 2
    return {"stn": z // 2 * (SIDE * SIDE) + y * SIDE + x, "freq": z % 2, "pts": core}


def at_multiple(index, size, length):
    return pl.ds(pl.multiple_of(index * size, size), length)


def kernel(
    greens,
    weights,
    out,
    own,
    near,
    far,
    transit,
    mix,
    parts,
    total,
    sums,
    g_send,
    g_recv,
    near_send,
    near_recv,
    hop_send,
    hop_recv,
    far_send,
    far_recv,
    wz_send,
    wz_recv,
    wx_send,
    wx_recv,
    wt_send,
    wt_recv,
    sum_send,
    sum_recv,
    row_send,
    row_recv,
):
    here = place()
    x, y, z, core = here

    barrier = pltpu.get_barrier_semaphore()
    for step in PARTNERS:
        pl.semaphore_signal(barrier, inc=1, device_id=device(here, *step), device_id_type=MESH)
    pl.semaphore_wait(barrier, len(PARTNERS))

    sent = []

    def send(src, dst, send_sem, recv_sem, step):
        copy = pltpu.make_async_remote_copy(
            src_ref=src,
            dst_ref=dst,
            send_sem=send_sem,
            recv_sem=recv_sem,
            device_id=device(here, *step),
            device_id_type=MESH,
        )
        copy.start()
        sent.append(copy)

    def arrived(dst, sem):
        pltpu.make_async_remote_copy(
            src_ref=dst,
            dst_ref=dst,
            send_sem=sem,
            recv_sem=sem,
            device_id=device(here, 1),
            device_id_type=MESH,
        ).wait_recv()

    def rank(dx, dz):
        return (z + dz) % SIDE // 2 * SIDE + (x + dx) % SIDE

    def rows(index):
        return at_multiple(index, RUN, RUN)

    mine = rank(0, 0)
    half = at_multiple(core, HALF, HALF)

    def send_greens(dx, dz):
        kept = (z + dz) % SIDE // 2
        send(
            greens.at[:, kept, :, at_multiple((x + dx) % SIDE, POINTS, POINTS)],
            own.at[:, rows(mine), :],
            g_send.at[SPREAD.index((dx, 0, dz, 0))],
            g_recv.at[mine],
            (dx, 0, dz),
        )

    def send_weights(dz):
        kept = (z + dz) % SIDE // 2
        for d in range(3):
            send(
                weights.at[:, kept, :, at_multiple(core * SIDE + (y + d) % SIDE, HALF, HALF)],
                mix.at[:, d, rows(mine), half],
                wz_send.at[dz // 2, d],
                wz_recv.at[z // 2, d],
                (0, 0, dz),
            )

    for dz in (1, 3):
        send_greens(0, dz)
    for dz in (1, 3):
        send_weights(dz)
    for dx in (1, 3, 2):
        for dz in (1, 3):
            send_greens(dx, dz)

    def mix_at(index):
        return mix.at[:, :, rows(index), half]

    def to_twin(index, slot):
        send(mix_at(index), mix_at(index), wt_send.at[slot], wt_recv.at[index], (0, 0, 0, 1))

    def green_piece(dx, dz):
        index = rank(dx, dz)
        slot = SPREAD.index((dx, 0, dz, 0))
        piece = own.at[:, rows(index), :]
        arrived(piece, g_recv.at[index])
        send(piece, near.at[:, rows(index), :], near_send.at[slot], near_recv.at[index], (0, 3, 0))
        other = at_multiple((y + 2) % SIDE // 2, HALF, HALF)
        send(
            own.at[:, rows(index), other],
            transit.at[:, rows(index), :],
            hop_send.at[slot],
            hop_recv.at[index],
            (0, 1, 0),
        )

    def pass_on(dx, dz):
        index = rank(dx, dz)
        slot = SPREAD.index((dx, 0, dz, 0))
        piece = transit.at[:, rows(index), :]
        arrived(piece, hop_recv.at[index])
        send(piece, far.at[:, rows(index), :], far_send.at[slot], far_recv.at[index], (0, 1, 0))

    for dz in (1, 3):
        green_piece(0, dz)
    for dz in (1, 3):
        zs = (z + dz) % SIDE // 2
        for d in range(3):
            arrived(mix.at[:, d, rows(rank(0, dz)), half], wz_recv.at[zs, d])
        index = rank(0, dz)
        for k, dx in enumerate((1, 3)):
            send(mix_at(index), mix_at(index), wx_send.at[k, dz // 2], wx_recv.at[index], (dx, 0, 0))
        to_twin(index, dz // 2)
    for dx in (1, 3):
        for dz in (1, 3):
            green_piece(dx, dz)
    for dz in (1, 3):
        pass_on(0, dz)
    for k, dx in enumerate((1, 3)):
        for zs in range(2):
            index = zs * SIDE + (x + dx) % SIDE
            arrived(mix_at(index), wx_recv.at[index])
            if zs == k:
                send(mix_at(index), mix_at(index), wx_send.at[2, k], wx_recv.at[index], (-dx % SIDE, 0, 0))
            to_twin(index, 2 + k * 2 + zs)
    for dz in (1, 3):
        green_piece(2, dz)
    for dx in (1, 3, 2):
        for dz in (1, 3):
            pass_on(dx, dz)
    for zs in range(2):
        index = zs * SIDE + (x + 2) % SIDE
        arrived(mix_at(index), wx_recv.at[index])
        to_twin(index, 6 + zs)
    for index in range(2 * SIDE):
        arrived(mix.at[:, :, rows(index), at_multiple(1 - core, HALF, HALF)], wt_recv.at[index])

    total[...] = jnp.zeros_like(total)

    def add_block(d, others, at_others, at_own, columns, weight):
        gr, gi = others[0, :, at_others], others[1, :, at_others]
        partial = jnp.zeros((8, HALF), jnp.float32)
        for m in range(0, BLOCK, HALF):
            wr, wi = mix[0, d, m : m + HALF, :], mix[1, d, m : m + HALF, :]

            def dot(a, b):
                return jnp.dot(a, b, preferred_element_type=jnp.float32)

            re = dot(wr, gr) - dot(wi, gi)
            im = dot(wr, gi) + dot(wi, gr)
            a = own[0, m : m + HALF, at_own].astype(jnp.float32)
            b = own[1, m : m + HALF, at_own].astype(jnp.float32)
            partial = partial + jnp.sum((a * re + b * im).reshape(HALF // 8, 8, HALF), axis=0)
        total[:, columns] += weight * partial

    for n in range(0, POINTS, HALF):
        span = slice(n, n + HALF)
        add_block(0, own, span, span, span, 1.0)
    for index in range(2 * SIDE):
        arrived(near.at[:, rows(index), :], near_recv.at[index])
    for n in range(0, POINTS, HALF):
        span = slice(n, n + HALF)
        add_block(1, near, span, span, span, 2.0)
    for index in range(2 * SIDE):
        arrived(far.at[:, rows(index), :], far_recv.at[index])
    here_half = at_multiple(y // 2, HALF, HALF)
    add_block(2, far, slice(0, HALF), here_half, here_half, 2.0)

    place_in_plane = z * SIDE + y
    stations = 2 * SIDE * SIDE * RUN
    parts[place_in_plane] = jnp.sum(total[...], axis=0, keepdims=True) / stations
    for k, step in enumerate(PLANE):
        mine_part = parts.at[place_in_plane]
        send(mine_part, mine_part, sum_send.at[k], sum_recv.at[place_in_plane], step)
    for _, dy, dz, _ in PLANE:
        slot = (z + dz) % SIDE * SIDE + (y + dy) % SIDE
        arrived(parts.at[slot], sum_recv.at[slot])
    raw = parts[0]
    for slot in range(1, SIDE * SIDE):
        raw = raw + parts[slot]
    place_in_row = core * SIDE + x
    sums[place_in_row] = raw
    for k, step in enumerate(ROW):
        mine_sum = sums.at[place_in_row]
        send(mine_sum, mine_sum, row_send.at[k], row_recv.at[place_in_row], step)
    for dx, _, _, dc in ROW:
        slot = (core + dc) % 2 * SIDE + (x + dx) % SIDE
        arrived(sums.at[slot], row_recv.at[slot])
    largest = jnp.max(jnp.abs(sums[...]))
    for k in range(SIDE):
        out[k] = sums[core * SIDE + k] / (largest + 1e-06)
    for copy in sent:
        copy.wait_send()


def body(greens, noise_weights):
    dma = pltpu.SemaphoreType.DMA
    spread, plane, row = len(SPREAD), len(PLANE), len(ROW)
    ranks = 2 * SIDE
    kernel_of_points = pl.pallas_call(
        kernel,
        out_shape=jax.ShapeDtypeStruct((SIDE, 1, POINTS), jnp.float32),
        in_specs=[pl.BlockSpec(memory_space=pl.ANY)] * 2,
        out_specs=pl.BlockSpec(memory_space=pltpu.VMEM),
        scratch_shapes=[
            pltpu.VMEM((2, BLOCK, POINTS), jnp.bfloat16),
            pltpu.VMEM((2, BLOCK, POINTS), jnp.bfloat16),
            pltpu.VMEM((2, BLOCK, HALF), jnp.bfloat16),
            pltpu.VMEM((2, BLOCK, HALF), jnp.bfloat16),
            pltpu.VMEM((2, 3, BLOCK, BLOCK), jnp.bfloat16),
            pltpu.VMEM((SIDE * SIDE, 1, POINTS), jnp.float32),
            pltpu.VMEM((8, POINTS), jnp.float32),
            pltpu.VMEM((ranks, 1, POINTS), jnp.float32),
            dma((spread,)),
            dma((ranks,)),
            dma((spread,)),
            dma((ranks,)),
            dma((spread,)),
            dma((ranks,)),
            dma((spread,)),
            dma((ranks,)),
            dma((2, 3)),
            dma((2, 3)),
            dma((3, 2)),
            dma((ranks,)),
            dma((ranks,)),
            dma((ranks,)),
            dma((plane,)),
            dma((plane + 1,)),
            dma((row,)),
            dma((row + 1,)),
        ],
        compiler_params=pltpu.CompilerParams(
            collective_id=0, has_side_effects=True, vmem_limit_bytes=48 * 2**20
        ),
    )(greens, noise_weights)
    return kernel_of_points.reshape(SIDE * POINTS)


def solution(mesh):
    in_specs = (P(None, "freq", "stn", "pts"), P(None, "freq", "stn", None))
    out_specs = P("pts")
    return jax.shard_map(body, mesh=mesh, in_specs=in_specs, out_specs=out_specs, check_vma=False)
```

time: 322 us -> 61.3 us (0.19)
  waiting for transfers between devices: 265 us -> 0 us
  Pallas kernels: 0 us -> 58 us
  blocking collectives: 23.5 us -> 0 us
  between operations: 14.1 us -> 0.01 us
  matrix products: 13 us -> 0 us
    all_gather x1 -> x0, waiting for transfers between devices: 265 us -> none  [body(): lax.all_gather(greens, 'stn', axis=2, tiled=True)]
    pallas_call x0 -> x1, Pallas kernels: none -> 58 us  [body(): pl.pallas_call(kernel, out_shape=jax.ShapeDtypeStruct((SIDE, 1, POINTS),...]
    all_to_all x2 -> x0, blocking collectives: 23.5 us -> none  [from_everyone(): lax.all_to_all(jnp.broadcast_to(x[None], (size, *x.shape)), axis, 0, 0, t...]
    dot_general x1 -> x0, matrix products: 13 us -> none  [body(): jnp.einsum('ocfin,cfnx->ofix', mixing, lax.all_gather(greens, 'stn', axis...]
  transfers between devices with their start and end apart: 1 -> 0, of which waited for: 1 -> 0; matrix products, arithmetic and copies ran while one was open for 0% -> 0% of each run, Pallas kernels for 0% -> 0%
where the time goes in v1:
time: 61.3 us; the launch traced here: 61.1 us
  Pallas kernels  58 us (95%)
  local copies, waits for them, and re-layouts  3.05 us (5%)
    pallas_call x1, Pallas kernels, body(): pl.pallas_call(kernel, out_shape=jax.ShapeDtypeStruct((SIDE, 1, POINTS),...  58 us
    unnamed x5, local copies, waits for them, and re-layouts  3.05 us

profile of v1, /device:TPU:1, one launch (start us, length us, event | category | flops | bytes accessed | tf_op | source)
XLA Modules:
  0.0 61.1 jit_solution(13957027284187331002)
XLA Ops:
  0.0 0.0 copy-start
  0.0 1.2 %copy-done = bf16[2,2,64,2048]{3,2,1,0:T(8,128)(2,1)S(1)} copy-done((bf16[2,2,64,2048]{3,2,1,0:T(8,128)(2,1)S(1)}, bf16[2,2,64,2048]{3,2,1,0:T(8,128)(2,1)}, u32[]{:S(2)}) %copy-start) | copy-done | bytes 1048600
  1.2 0.0 copy-start.1
  1.2 1.2 %copy-done.1 = bf16[2,2,64,2048]{3,2,1,0:T(8,128)(2,1)S(1)} copy-done((bf16[2,2,64,2048]{3,2,1,0:T(8,128)(2,1)S(1)}, bf16[2,2,64,2048]{3,2,1,0:T(8,128)(2,1)}, u32[]{:S(2)}) %copy-start.1) | copy-done | bytes 1048600
  2.5 58.0 %shard_map.28 = f32[4,1,512]{2,1,0:T(1,128)S(1)} custom-call(bf16[2,2,64,2048]{3,2,1,0:T(8,128)(2,1)S(1)} %copy-done, bf16[2,2,64,2048]{3,2,1,0:T(8,128)(2,1)S(1)} %copy-done.1), custom_call_target="tpu_custom_call" | custom-call | tf_op jit(solution)/shard_map/pallas_call | solution.py:263
  60.5 0.6 copy.4
Async XLA Ops:
  0.0 1.2 %copy-start = (bf16[2,2,64,2048]{3,2,1,0:T(8,128)(2,1)S(1)}, bf16[2,2,64,2048]{3,2,1,0:T(8,128)(2,1)}, u32[]{:S(2)}) copy-start(bf16[2,2,64,2048]{3,2,1,0:T(8,128)(2,1)} %greens.1) | copy-start | bytes 3145732
  1.2 1.2 %copy-start.1 = (bf16[2,2,64,2048]{3,2,1,0:T(8,128)(2,1)S(1)}, bf16[2,2,64,2048]{3,2,1,0:T(8,128)(2,1)}, u32[]{:S(2)}) copy-start(bf16[2,2,64,2048]{3,2,1,0:T(8,128)(2,1)} %weights.1) | copy-start | bytes 3145732

commit v2 on v1

v2 whole, which is shorter than its diff:
```python
import jax
import jax.numpy as jnp
from jax import lax
from jax.experimental import pallas as pl
from jax.experimental.pallas import tpu as pltpu
from jax.sharding import PartitionSpec as P

MESH = pl.DeviceIdType.MESH
SIDE = 4
RUN = 64
BLOCK = 512
POINTS = 512
HALF = 256

SPREAD = [(dx, 0, dz, 0) for dx in (0, 1, 3, 2) for dz in (1, 3)]
PLANE = [(0, dy, dz, 0) for dz in range(SIDE) for dy in range(SIDE) if dy or dz]
ROW = [(dx, 0, 0, dc) for dx in range(SIDE) for dc in range(2) if dx or dc]
OUTGOING = [(0, 1), (0, 3), (1, 3), (3, 3), (1, 1), (3, 1), (2, 3), (2, 1)]
NEAREST = [(1, 0, 0), (3, 0, 0), (2, 0, 0), (0, 1, 0), (0, 3, 0), (0, 0, 1), (0, 0, 3), (0, 0, 0, 1)]


def place():
    stn = lax.axis_index("stn")
    x, y = stn % SIDE, stn // SIDE % SIDE
    z = stn // (SIDE * SIDE) * 2 + lax.axis_index("freq")
    return x, y, z, lax.axis_index("pts")


def device(here, dx=0, dy=0, dz=0, dc=0):
    x, y, z, core = here
    x, y, z, core = (x + dx) % SIDE, (y + dy) % SIDE, (z + dz) % SIDE, (core + dc) % 2
    return {"stn": z // 2 * (SIDE * SIDE) + y * SIDE + x, "freq": z % 2, "pts": core}


def at_multiple(index, size, length):
    return pl.ds(pl.multiple_of(index * size, size), length)


def kernel(
    greens,
    weights,
    out,
    own,
    near,
    far,
    transit,
    mix,
    parts,
    total,
    sums,
    g_send,
    g_recv,
    near_send,
    near_recv,
    hop_send,
    hop_recv,
    far_send,
    far_recv,
    wz_send,
    wz_recv,
    wx_send,
    wx_recv,
    wt_send,
    wt_recv,
    sum_send,
    sum_recv,
    row_send,
    row_recv,
    greens_here,
    weights_here,
    load,
    stage_x,
    stage_z,
    stage_recv,
    forward_send,
):
    here = place()
    x, y, z, core = here

    barrier = pltpu.get_barrier_semaphore()
    for step in NEAREST:
        pl.semaphore_signal(barrier, inc=1, device_id=device(here, *step), device_id_type=MESH)

    def at_greens(dx, dz):
        columns = at_multiple((x + dx) % SIDE, POINTS, POINTS)
        return slice(None), (z + dz) % SIDE // 2, slice(None), columns

    greens_in = {}
    for k, (dx, dz) in enumerate(OUTGOING):
        part = at_greens(dx, dz)
        greens_in[dx, dz] = pltpu.make_async_copy(greens.at[part], greens_here.at[k], load.at[k])
        greens_in[dx, dz].start()
    for d in range(3):
        columns = at_multiple(core * SIDE + (y + d) % SIDE, HALF, HALF)
        pltpu.make_async_copy(
            weights.at[:, :, :, columns], weights_here.at[:, :, d], load.at[len(OUTGOING)]
        ).start()
    pl.semaphore_wait(barrier, len(NEAREST))

    def send(src, dst, send_sem, recv_sem, step):
        copy = pltpu.make_async_remote_copy(
            src_ref=src,
            dst_ref=dst,
            send_sem=send_sem,
            recv_sem=recv_sem,
            device_id=device(here, *step),
            device_id_type=MESH,
        )
        copy.start()

    def arrived(dst, sem):
        pltpu.make_async_remote_copy(
            src_ref=dst,
            dst_ref=dst,
            send_sem=sem,
            recv_sem=sem,
            device_id=device(here, 1),
            device_id_type=MESH,
        ).wait_recv()

    def left(src, sem):
        pltpu.make_async_remote_copy(
            src_ref=src,
            dst_ref=src,
            send_sem=sem,
            recv_sem=sem,
            device_id=device(here, 1),
            device_id_type=MESH,
        ).wait_send()

    def rank(dx, dz):
        return (z + dz) % SIDE // 2 * SIDE + (x + dx) % SIDE

    def rows(index):
        return at_multiple(index, RUN, RUN)

    mine = rank(0, 0)
    half = at_multiple(core, HALF, HALF)

    def send_greens(dx, dz):
        piece = greens_here.at[OUTGOING.index((dx, dz))]
        greens_in[dx, dz].wait()
        if dx == 0:
            send(piece, own.at[:, rows(mine), :], g_send, g_recv.at[mine], (0, 0, dz))
        elif dz == 1:
            send(piece, stage_z.at[dx - 1], g_send, stage_recv.at[0, dx - 1], (0, 0, dz))
        else:
            send(piece, stage_x.at[dx - 1], g_send, stage_recv.at[1, dx - 1], (dx, 0, 0))

    def forward_x(dx):
        piece, index = stage_z.at[dx - 1], rank(0, 3)
        arrived(piece, stage_recv.at[0, dx - 1])
        send(piece, own.at[:, rows(index), :], forward_send, g_recv.at[index], (dx, 0, 0))

    def forward_z(dx):
        piece, index = stage_x.at[dx - 1], rank(-dx, 0)
        arrived(piece, stage_recv.at[1, dx - 1])
        send(piece, own.at[:, rows(index), :], forward_send, g_recv.at[index], (0, 0, 3))

    def send_weights(dz, d):
        kept = (z + dz) % SIDE // 2
        send(
            weights_here.at[:, kept, d],
            mix_at(mine, d),
            wz_send,
            wz_recv.at[z // 2, d],
            (0, 0, dz),
        )

    def mix_at(index, d):
        return mix.at[:, d, rows(index), half]

    def to_twin(index, d, dz):
        piece = mix_at(index, d)
        send(piece, piece, wt_send, wt_recv.at[dz // 2, d], (0, 0, 0, 1))

    def green_piece(dx, dz):
        index = rank(dx, dz)
        piece = own.at[:, rows(index), :]
        arrived(piece, g_recv.at[index])
        send(piece, near.at[:, rows(index), :], near_send, near_recv, (0, 3, 0))
        other = at_multiple((y + 2) % SIDE // 2, HALF, HALF)
        send(
            own.at[:, rows(index), other],
            transit.at[:, rows(index), :],
            hop_send,
            hop_recv.at[index],
            (0, 1, 0),
        )

    def pass_on(dx, dz):
        index = rank(dx, dz)
        piece = transit.at[:, rows(index), :]
        arrived(piece, hop_recv.at[index])
        send(piece, far.at[:, rows(index), :], far_send, far_recv, (0, 1, 0))

    def weights_along_z(d, dz):
        index = rank(0, dz)
        piece = mix_at(index, d)
        arrived(piece, wz_recv.at[(z + dz) % SIDE // 2, d])
        for dx in (1, 3):
            send(piece, piece, wx_send, wx_recv.at[SIDE - dx - 1, dz // 2, d], (dx, 0, 0))
        to_twin(index, d, dz)

    def weights_along_x(d, dz):
        for k, dx in enumerate((1, 3)):
            index = rank(dx, dz)
            piece = mix_at(index, d)
            arrived(piece, wx_recv.at[dx - 1, dz // 2, d])
            if dz // 2 == k:
                send(piece, piece, wx_send, wx_recv.at[1, dz // 2, d], (-dx % SIDE, 0, 0))
            to_twin(index, d, dz)

    def weights_across(d, dz):
        index = rank(2, dz)
        arrived(mix_at(index, d), wx_recv.at[1, dz // 2, d])
        to_twin(index, d, dz)

    def weights_from_twin(d, dz):
        part = at_multiple((z + dz) % SIDE // 2, HALF, HALF)
        arrived(mix.at[:, d, part, at_multiple(1 - core, HALF, HALF)], wt_recv.at[dz // 2, d])

    total[...] = jnp.zeros_like(total)

    def add_block(d, dz, others, at_others, at_own, columns, weight):
        gr, gi = others[0, :, at_others], others[1, :, at_others]
        part = at_multiple((z + dz) % SIDE // 2, HALF, HALF)
        wr, wi = mix[0, d, part, :], mix[1, d, part, :]

        def dot(a, b):
            return jnp.dot(a, b, preferred_element_type=jnp.float32)

        re = dot(wr, gr) - dot(wi, gi)
        im = dot(wr, gi) + dot(wi, gr)
        a = own[0, part, at_own].astype(jnp.float32)
        b = own[1, part, at_own].astype(jnp.float32)
        partial = jnp.sum((a * re + b * im).reshape(HALF // 8, 8, HALF), axis=0)
        total[:, columns] += weight * partial

    def add_whole(d, dz, others, weight):
        weights_from_twin(d, dz)
        for n in range(0, POINTS, HALF):
            span = slice(n, n + HALF)
            add_block(d, dz, others, span, span, span, weight)

    for dz in (1, 3):
        send_greens(0, dz)
    for dx in (1, 3, 2):
        send_greens(dx, 3)
    pltpu.make_async_copy(weights_here, weights_here, load.at[len(OUTGOING)]).wait()
    send_weights(3, 0)
    send_greens(1, 1)
    send_weights(3, 1)
    send_greens(3, 1)
    send_weights(3, 2)
    send_greens(2, 1)
    for d in range(3):
        send_weights(1, d)
    green_piece(0, 1)
    green_piece(0, 3)
    forward_z(1)
    forward_z(3)
    weights_along_z(0, 1)
    weights_along_z(1, 1)
    forward_x(1)
    weights_along_z(2, 1)
    pass_on(0, 1)
    forward_z(2)
    pass_on(0, 3)
    forward_x(3)
    green_piece(3, 1)
    weights_along_x(0, 1)
    green_piece(1, 3)
    green_piece(1, 1)
    forward_x(2)
    weights_along_x(1, 1)
    green_piece(3, 3)
    weights_along_z(0, 3)
    weights_along_x(2, 1)
    pass_on(3, 1)
    green_piece(2, 1)
    weights_along_z(1, 3)
    weights_along_z(2, 3)
    weights_across(0, 1)
    green_piece(2, 3)
    pass_on(1, 3)
    weights_across(1, 1)
    pass_on(1, 1)
    pass_on(3, 3)
    weights_across(2, 1)
    weights_along_x(0, 3)
    weights_along_x(1, 3)
    pass_on(2, 1)
    weights_along_x(2, 3)
    add_whole(0, 1, own, 1.0)
    weights_across(0, 3)
    weights_across(1, 3)
    weights_across(2, 3)
    pass_on(2, 3)
    add_whole(0, 3, own, 1.0)
    arrived(near, near_recv)
    add_whole(1, 1, near, 2.0)
    add_whole(1, 3, near, 2.0)
    arrived(far, far_recv)
    here_half = at_multiple(y // 2, HALF, HALF)
    for dz in (1, 3):
        weights_from_twin(2, dz)
        add_block(2, dz, far, slice(0, HALF), here_half, here_half, 2.0)

    place_in_plane = z * SIDE + y
    stations = 2 * SIDE * SIDE * RUN
    parts[place_in_plane] = jnp.sum(total[...], axis=0, keepdims=True) / stations
    for step in PLANE:
        mine_part = parts.at[place_in_plane]
        send(mine_part, mine_part, sum_send, sum_recv, step)
    arrived(parts.at[: len(PLANE)], sum_recv)
    raw = parts[0]
    for slot in range(1, SIDE * SIDE):
        raw = raw + parts[slot]
    place_in_row = core * SIDE + x
    sums[place_in_row] = raw
    for step in ROW:
        mine_sum = sums.at[place_in_row]
        send(mine_sum, mine_sum, row_send, row_recv, step)
    arrived(sums.at[: len(ROW)], row_recv)
    largest = jnp.max(jnp.abs(sums[...]))
    for k in range(SIDE):
        out[k] = sums[core * SIDE + k] / (largest + 1e-06)
    left(own, g_send)
    left(own.at[:, : 6 * RUN, :], forward_send)
    left(own, near_send)
    left(transit, hop_send)
    left(far, far_send)
    left(mix.at[:, :, : 2 * RUN, half], wz_send)
    left(mix.at[:, :, : 6 * RUN, half], wx_send)
    left(mix.at[:, :, :, half], wt_send)
    left(parts.at[: len(PLANE)], sum_send)
    left(sums.at[: len(ROW)], row_send)


def body(greens, noise_weights):
    dma = pltpu.SemaphoreType.DMA
    spread = len(SPREAD)
    ranks = 2 * SIDE
    kernel_of_points = pl.pallas_call(
        kernel,
        out_shape=jax.ShapeDtypeStruct((SIDE, 1, POINTS), jnp.float32),
        in_specs=[pl.BlockSpec(memory_space=pl.ANY)] * 2,
        out_specs=pl.BlockSpec(memory_space=pltpu.VMEM),
        scratch_shapes=[
            pltpu.VMEM((2, BLOCK, POINTS), jnp.bfloat16),
            pltpu.VMEM((2, BLOCK, POINTS), jnp.bfloat16),
            pltpu.VMEM((2, BLOCK, HALF), jnp.bfloat16),
            pltpu.VMEM((2, BLOCK, HALF), jnp.bfloat16),
            pltpu.VMEM((2, 3, BLOCK, BLOCK), jnp.bfloat16),
            pltpu.VMEM((SIDE * SIDE, 1, POINTS), jnp.float32),
            pltpu.VMEM((8, POINTS), jnp.float32),
            pltpu.VMEM((ranks, 1, POINTS), jnp.float32),
            dma,
            dma((ranks,)),
            dma,
            dma,
            dma,
            dma((ranks,)),
            dma,
            dma,
            dma,
            dma((2, 3)),
            dma,
            dma((3, 2, 3)),
            dma,
            dma((2, 3)),
            dma,
            dma,
            dma,
            dma,
            pltpu.VMEM((spread, 2, RUN, POINTS), jnp.bfloat16),
            pltpu.VMEM((2, 2, 3, RUN, HALF), jnp.bfloat16),
            dma((spread + 1,)),
            pltpu.VMEM((3, 2, RUN, POINTS), jnp.bfloat16),
            pltpu.VMEM((3, 2, RUN, POINTS), jnp.bfloat16),
            dma((2, 3)),
            dma,
        ],
        compiler_params=pltpu.CompilerParams(
            collective_id=0, has_side_effects=True, vmem_limit_bytes=213 * 2**18
        ),
    )(greens, noise_weights)
    return kernel_of_points.reshape(SIDE * POINTS)


def solution(mesh):
    in_specs = (P(None, "freq", "stn", "pts"), P(None, "freq", "stn", None))
    out_specs = P("pts")
    return jax.shard_map(body, mesh=mesh, in_specs=in_specs, out_specs=out_specs, check_vma=False)
```

time: 61.3 us -> 51.2 us (0.84)
  Pallas kernels: 58 us -> 50.5 us
  local copies, waits for them, and re-layouts: 3.05 us -> 0.6 us
    pallas_call x1, Pallas kernels: 58 us -> 50.5 us  [body(): pl.pallas_call(kernel, out_shape=jax.ShapeDtypeStruct((SIDE, 1, POINTS),...]
    unnamed x5 -> x1, local copies, waits for them, and re-layouts: 3.05 us -> 0.6 us
where the time goes in v2:
time: 51.2 us; the launch traced here: 51.1 us
  Pallas kernels  50.5 us (99%)
  local copies, waits for them, and re-layouts  0.6 us (1%)
    pallas_call x1, Pallas kernels, body(): pl.pallas_call(kernel, out_shape=jax.ShapeDtypeStruct((SIDE, 1, POINTS),...  50.5 us

profile of v2, /device:TPU:1, one launch (start us, length us, event | category | flops | bytes accessed | tf_op | source)
XLA Modules:
  0.0 51.1 jit_solution(2692162685821756353)
XLA Ops:
  0.0 50.5 %shard_map.28 = f32[4,1,512]{2,1,0:T(1,128)S(1)} custom-call(bf16[2,2,64,2048]{3,2,1,0:T(8,128)(2,1)} %greens.1, bf16[2,2,64,2048]{3,2,1,0:T(8,128)(2,1)} %weights.1), custom_call_target="tpu_custom_call" | custom-call | tf_op jit(solution)/shard_map/pallas_call | solution.py:345
  50.5 0.6 %copy.4 = f32[2048]{0:T(1024)} copy(f32[2048]{0:T(1024)S(1)} %bitcast.1) | data formatting | bytes 16384

commit v3 on v2

--- a/solution.py
+++ b/solution.py
@@ -43,7 +43,7 @@
     own,
     near,
     far,
-    transit,
+    stage_w,
     mix,
     parts,
     total,
@@ -52,8 +52,8 @@
     g_recv,
     near_send,
     near_recv,
-    hop_send,
-    hop_recv,
+    wy_send,
+    wy_recv,
     far_send,
     far_recv,
     wz_send,
@@ -73,6 +73,7 @@
     stage_z,
     stage_recv,
     forward_send,
+    met,
 ):
     here = place()
     x, y, z, core = here
@@ -90,11 +91,20 @@
         part = at_greens(dx, dz)
         greens_in[dx, dz] = pltpu.make_async_copy(greens.at[part], greens_here.at[k], load.at[k])
         greens_in[dx, dz].start()
-    for d in range(3):
-        columns = at_multiple(core * SIDE + (y + d) % SIDE, HALF, HALF)
-        pltpu.make_async_copy(
-            weights.at[:, :, :, columns], weights_here.at[:, :, d], load.at[len(OUTGOING)]
-        ).start()
+
+    brings = pl.when(core == 1)
+
+    @brings
+    def load_weights():
+        for d in range(3):
+            for zs in range(2):
+                columns = at_multiple(zs * SIDE + (y + d) % SIDE, HALF, HALF)
+                pltpu.make_async_copy(
+                    weights.at[:, :, :, columns],
+                    weights_here.at[:, :, d, :, zs * HALF : (zs + 1) * HALF],
+                    load.at[len(OUTGOING)],
+                ).start()
+
     pl.semaphore_wait(barrier, len(NEAREST))
 
     def send(src, dst, send_sem, recv_sem, step):
@@ -135,7 +145,9 @@
         return at_multiple(index, RUN, RUN)
 
     mine = rank(0, 0)
-    half = at_multiple(core, HALF, HALF)
+
+    def half(dz):
+        return at_multiple((z + dz) % SIDE // 2, HALF, HALF)
 
     def send_greens(dx, dz):
         piece = greens_here.at[OUTGOING.index((dx, dz))]
@@ -159,153 +171,197 @@
 
     def send_weights(dz, d):
         kept = (z + dz) % SIDE // 2
-        send(
-            weights_here.at[:, kept, d],
-            mix_at(mine, d),
-            wz_send,
-            wz_recv.at[z // 2, d],
-            (0, 0, dz),
-        )
-
-    def mix_at(index, d):
-        return mix.at[:, d, rows(index), half]
+        columns = columns_of(d, -dz % SIDE, z // 2)
+
+        @brings
+        def to_neighbour():
+            send(
+                weights_here.at[:, kept, d, :, columns],
+                stage_w.at[-dz % SIDE // 2] if d == 2 else mix.at[:, d, rows(mine), columns],
+                wz_send,
+                wz_recv.at[-dz % SIDE // 2, d],
+                (0, 0, dz),
+            )
+
+    def columns_of(d, dz, zs):
+        return at_multiple(zs, HALF, HALF) if d == 0 and dz == 3 else slice(None)
+
+    def mix_at(index, d, dz):
+        return mix.at[:, d, rows(index), columns_of(d, dz, (z + dz) % SIDE // 2)]
 
     def to_twin(index, d, dz):
-        piece = mix_at(index, d)
-        send(piece, piece, wt_send, wt_recv.at[dz // 2, d], (0, 0, 0, 1))
+        piece = mix_at(index, d, dz)
+        send(piece, piece, wt_send.at[d], wt_recv.at[dz // 2, d], (0, 0, 0, 1))
 
     def green_piece(dx, dz):
         index = rank(dx, dz)
         piece = own.at[:, rows(index), :]
         arrived(piece, g_recv.at[index])
-        send(piece, near.at[:, rows(index), :], near_send, near_recv, (0, 3, 0))
-        other = at_multiple((y + 2) % SIDE // 2, HALF, HALF)
-        send(
-            own.at[:, rows(index), other],
-            transit.at[:, rows(index), :],
-            hop_send,
-            hop_recv.at[index],
-            (0, 1, 0),
-        )
-
-    def pass_on(dx, dz):
-        index = rank(dx, dz)
-        piece = transit.at[:, rows(index), :]
-        arrived(piece, hop_recv.at[index])
-        send(piece, far.at[:, rows(index), :], far_send, far_recv, (0, 1, 0))
-
-    def weights_along_z(d, dz):
-        index = rank(0, dz)
-        piece = mix_at(index, d)
-        arrived(piece, wz_recv.at[(z + dz) % SIDE // 2, d])
+        send(piece, near.at[:, rows(index), :], near_send, near_recv.at[dz // 2], (0, 3, 0))
+        other = at_multiple((y + 1) % SIDE // 2, HALF, HALF)
+        send(own.at[:, rows(index), other], far.at[:, rows(index), :], far_send, far_recv, (0, 1, 0))
+
+    def spread_weights(index, d, dz):
+        piece = mix_at(index, d, dz)
         for dx in (1, 3):
             send(piece, piece, wx_send, wx_recv.at[SIDE - dx - 1, dz // 2, d], (dx, 0, 0))
         to_twin(index, d, dz)
 
+    def weights_along_z(d, dz):
+        @brings
+        def onward():
+            index = rank(0, dz)
+            if d == 2:
+                piece = stage_w.at[dz // 2]
+                arrived(piece, wz_recv.at[dz // 2, d])
+                send(piece, mix_at(index, d, dz), wy_send, wy_recv.at[dz // 2], (0, 1, 0))
+            else:
+                arrived(mix_at(index, d, dz), wz_recv.at[dz // 2, d])
+                spread_weights(index, d, dz)
+
+    def weights_along_y(dz):
+        @brings
+        def onward():
+            index = rank(0, dz)
+            arrived(mix_at(index, 2, dz), wy_recv.at[dz // 2])
+            spread_weights(index, 2, dz)
+
     def weights_along_x(d, dz):
-        for k, dx in enumerate((1, 3)):
-            index = rank(dx, dz)
-            piece = mix_at(index, d)
-            arrived(piece, wx_recv.at[dx - 1, dz // 2, d])
-            if dz // 2 == k:
-                send(piece, piece, wx_send, wx_recv.at[1, dz // 2, d], (-dx % SIDE, 0, 0))
+        @brings
+        def spread_out():
+            for k, dx in enumerate((1, 3)):
+                index = rank(dx, dz)
+                piece = mix_at(index, d, dz)
+                arrived(piece, wx_recv.at[dx - 1, dz // 2, d])
+                if dz // 2 == k:
+                    send(piece, piece, wx_send, wx_recv.at[1, dz // 2, d], (-dx % SIDE, 0, 0))
+                to_twin(index, d, dz)
+
+    def weights_across(d, dz):
+        @brings
+        def hand_over():
+            index = rank(2, dz)
+            arrived(mix_at(index, d, dz), wx_recv.at[1, dz // 2, d])
             to_twin(index, d, dz)
 
-    def weights_across(d, dz):
-        index = rank(2, dz)
-        arrived(mix_at(index, d), wx_recv.at[1, dz // 2, d])
-        to_twin(index, d, dz)
-
     def weights_from_twin(d, dz):
-        part = at_multiple((z + dz) % SIDE // 2, HALF, HALF)
-        arrived(mix.at[:, d, part, at_multiple(1 - core, HALF, HALF)], wt_recv.at[dz // 2, d])
+        @pl.when(core == 0)
+        def take():
+            columns = columns_of(d, dz, (z + dz) % SIDE // 2)
+            arrived(mix.at[:, d, : SIDE * RUN, columns], wt_recv.at[dz // 2, d])
 
     total[...] = jnp.zeros_like(total)
 
-    def add_block(d, dz, others, at_others, at_own, columns, weight):
-        gr, gi = others[0, :, at_others], others[1, :, at_others]
-        part = at_multiple((z + dz) % SIDE // 2, HALF, HALF)
-        wr, wi = mix[0, d, part, :], mix[1, d, part, :]
-
-        def dot(a, b):
-            return jnp.dot(a, b, preferred_element_type=jnp.float32)
-
-        re = dot(wr, gr) - dot(wi, gi)
-        im = dot(wr, gi) + dot(wi, gr)
-        a = own[0, part, at_own].astype(jnp.float32)
-        b = own[1, part, at_own].astype(jnp.float32)
+    def add_block(d, dz, dj, firsts, at_firsts, others, at_others, columns, weight):
+        part = half(dz)
+
+        def product(at_j):
+            wr, wi = mix[0, d, part, at_j], mix[1, d, part, at_j]
+            gr, gi = others[0, at_j, at_others], others[1, at_j, at_others]
+
+            def dot(a, b):
+                return jnp.dot(a, b, preferred_element_type=jnp.float32)
+
+            return dot(wr, gr) - dot(wi, gi), dot(wr, gi) + dot(wi, gr)
+
+        if d:
+            re, im = product(half(dj))
+        else:
+            re, im = product(half(dz))
+            if dz == 1:
+                re2, im2 = product(half(3))
+                re, im = re + 2.0 * re2, im + 2.0 * im2
+        a = firsts[0, part, at_firsts].astype(jnp.float32)
+        b = firsts[1, part, at_firsts].astype(jnp.float32)
         partial = jnp.sum((a * re + b * im).reshape(HALF // 8, 8, HALF), axis=0)
         total[:, columns] += weight * partial
 
-    def add_whole(d, dz, others, weight):
-        weights_from_twin(d, dz)
+    def add_own(dz):
+        weights_from_twin(0, dz)
         for n in range(0, POINTS, HALF):
             span = slice(n, n + HALF)
-            add_block(d, dz, others, span, span, span, weight)
+            add_block(0, dz, None, own, span, own, span, span, 1.0)
+
+    def add_near(dz, dj):
+        for n in range(0, POINTS, HALF):
+            span = slice(n, n + HALF)
+            add_block(1, dz, dj, own, span, near, span, span, 2.0)
+
+    def add_far(dz, dj):
+        at_points = at_multiple(y // 2, HALF, HALF)
+        add_block(2, dz, dj, far, slice(None), near, at_points, at_points, 2.0)
 
     for dz in (1, 3):
         send_greens(0, dz)
     for dx in (1, 3, 2):
         send_greens(dx, 3)
-    pltpu.make_async_copy(weights_here, weights_here, load.at[len(OUTGOING)]).wait()
+
+    @brings
+    def weights_loaded():
+        pltpu.make_async_copy(weights_here, weights_here, load.at[len(OUTGOING)]).wait()
+
     send_weights(3, 0)
     send_greens(1, 1)
+    send_weights(1, 2)
+    send_greens(3, 1)
+    send_weights(1, 0)
+    send_weights(1, 1)
+    send_greens(2, 1)
+    send_weights(3, 2)
     send_weights(3, 1)
-    send_greens(3, 1)
-    send_weights(3, 2)
-    send_greens(2, 1)
-    for d in range(3):
-        send_weights(1, d)
     green_piece(0, 1)
     green_piece(0, 3)
+    pl.semaphore_signal(met, inc=1, device_id=device(here, 0, 3), device_id_type=MESH)
     forward_z(1)
     forward_z(3)
     weights_along_z(0, 1)
-    weights_along_z(1, 1)
     forward_x(1)
     weights_along_z(2, 1)
-    pass_on(0, 1)
+    weights_along_z(1, 1)
     forward_z(2)
-    pass_on(0, 3)
     forward_x(3)
     green_piece(3, 1)
     weights_along_x(0, 1)
+    weights_along_y(1)
+    weights_along_z(0, 3)
+    green_piece(3, 3)
+    weights_along_z(2, 3)
+    weights_along_x(1, 1)
+    weights_across(0, 1)
+    weights_along_z(1, 3)
+    green_piece(1, 1)
+    weights_along_x(2, 1)
+    forward_x(2)
     green_piece(1, 3)
-    green_piece(1, 1)
-    forward_x(2)
-    weights_along_x(1, 1)
-    green_piece(3, 3)
-    weights_along_z(0, 3)
-    weights_along_x(2, 1)
-    pass_on(3, 1)
+    weights_along_y(3)
+    weights_along_x(0, 3)
+    weights_across(1, 1)
     green_piece(2, 1)
-    weights_along_z(1, 3)
-    weights_along_z(2, 3)
-    weights_across(0, 1)
+    weights_across(2, 1)
+    weights_along_x(1, 3)
+    weights_across(0, 3)
+    pl.semaphore_wait(met, 1)
     green_piece(2, 3)
-    pass_on(1, 3)
-    weights_across(1, 1)
-    pass_on(1, 1)
-    pass_on(3, 3)
-    weights_across(2, 1)
-    weights_along_x(0, 3)
-    weights_along_x(1, 3)
-    pass_on(2, 1)
     weights_along_x(2, 3)
-    add_whole(0, 1, own, 1.0)
-    weights_across(0, 3)
     weights_across(1, 3)
+    add_own(1)
+    add_own(3)
+    weights_from_twin(1, 1)
+    weights_from_twin(1, 3)
+    arrived(near.at[:, half(1), :], near_recv.at[0])
+    add_near(1, 1)
+    add_near(3, 1)
+    weights_from_twin(2, 1)
+    arrived(far, far_recv)
+    add_far(1, 1)
+    arrived(near.at[:, half(3), :], near_recv.at[1])
+    add_near(1, 3)
+    add_near(3, 3)
+    add_far(1, 3)
     weights_across(2, 3)
-    pass_on(2, 3)
-    add_whole(0, 3, own, 1.0)
-    arrived(near, near_recv)
-    add_whole(1, 1, near, 2.0)
-    add_whole(1, 3, near, 2.0)
-    arrived(far, far_recv)
-    here_half = at_multiple(y // 2, HALF, HALF)
-    for dz in (1, 3):
-        weights_from_twin(2, dz)
-        add_block(2, dz, far, slice(0, HALF), here_half, here_half, 2.0)
+    weights_from_twin(2, 3)
+    add_far(3, 1)
+    add_far(3, 3)
 
     place_in_plane = z * SIDE + y
     stations = 2 * SIDE * SIDE * RUN
@@ -329,13 +385,18 @@
     left(own, g_send)
     left(own.at[:, : 6 * RUN, :], forward_send)
     left(own, near_send)
-    left(transit, hop_send)
     left(far, far_send)
-    left(mix.at[:, :, : 2 * RUN, half], wz_send)
-    left(mix.at[:, :, : 6 * RUN, half], wx_send)
-    left(mix.at[:, :, :, half], wt_send)
     left(parts.at[: len(PLANE)], sum_send)
     left(sums.at[: len(ROW)], row_send)
+
+    @brings
+    def weights_left():
+        left(mix.at[:, 0, : 11 * RUN // 2, :], wz_send)
+        left(mix.at[:, :, : 11 * RUN // 2, :], wx_send)
+        left(mix.at[:, 0, : 6 * RUN, :], wt_send.at[0])
+        left(mix.at[:, 1], wt_send.at[1])
+        left(mix.at[:, 2], wt_send.at[2])
+        left(mix.at[:, 0, : 2 * RUN, :], wy_send)
 
 
 def body(greens, noise_weights):
@@ -351,7 +412,7 @@
             pltpu.VMEM((2, BLOCK, POINTS), jnp.bfloat16),
             pltpu.VMEM((2, BLOCK, POINTS), jnp.bfloat16),
             pltpu.VMEM((2, BLOCK, HALF), jnp.bfloat16),
-            pltpu.VMEM((2, BLOCK, HALF), jnp.bfloat16),
+            pltpu.VMEM((2, 2, RUN, BLOCK), jnp.bfloat16),
             pltpu.VMEM((2, 3, BLOCK, BLOCK), jnp.bfloat16),
             pltpu.VMEM((SIDE * SIDE, 1, POINTS), jnp.float32),
             pltpu.VMEM((8, POINTS), jnp.float32),
@@ -359,28 +420,29 @@
             dma,
             dma((ranks,)),
             dma,
-            dma,
-            dma,
-            dma((ranks,)),
+            dma((2,)),
+            dma,
+            dma((2,)),
             dma,
             dma,
             dma,
             dma((2, 3)),
             dma,
             dma((3, 2, 3)),
-            dma,
+            dma((3,)),
             dma((2, 3)),
             dma,
             dma,
             dma,
             dma,
             pltpu.VMEM((spread, 2, RUN, POINTS), jnp.bfloat16),
-            pltpu.VMEM((2, 2, 3, RUN, HALF), jnp.bfloat16),
+            pltpu.VMEM((2, 2, 3, RUN, BLOCK), jnp.bfloat16),
             dma((spread + 1,)),
             pltpu.VMEM((3, 2, RUN, POINTS), jnp.bfloat16),
             pltpu.VMEM((3, 2, RUN, POINTS), jnp.bfloat16),
             dma((2, 3)),
             dma,
+            pltpu.SemaphoreType.REGULAR,
         ],
         compiler_params=pltpu.CompilerParams(
             collective_id=0, has_side_effects=True, vmem_limit_bytes=213 * 2**18

time: 51.2 us -> 50.5 us (0.986)
  Pallas kernels: 50.5 us -> 49.8 us
    pallas_call x1, Pallas kernels: 50.5 us -> 49.8 us  [body(): pl.pallas_call(kernel, out_shape=jax.ShapeDtypeStruct((SIDE, 1, POINTS),...]
where the time goes in v3:
time: 50.5 us; the launch traced here: 50.4 us
  Pallas kernels  49.8 us (99%)
  local copies, waits for them, and re-layouts  0.6 us (1%)
    pallas_call x1, Pallas kernels, body(): pl.pallas_call(kernel, out_shape=jax.ShapeDtypeStruct((SIDE, 1, POINTS),...  49.8 us

profile of v3, /device:TPU:1, one launch (start us, length us, event | category | flops | bytes accessed | tf_op | source)
XLA Modules:
  0.0 50.4 jit_solution(15137536480051402310)
XLA Ops:
  0.0 49.8 %shard_map.28 = f32[4,1,512]{2,1,0:T(1,128)S(1)} custom-call(bf16[2,2,64,2048]{3,2,1,0:T(8,128)(2,1)} %greens.1, bf16[2,2,64,2048]{3,2,1,0:T(8,128)(2,1)} %weights.1), custom_call_target="tpu_custom_call" | custom-call | tf_op jit(solution)/shard_map/pallas_call | solution.py:406
  49.8 0.6 %copy.4 = f32[2048]{0:T(1024)} copy(f32[2048]{0:T(1024)S(1)} %bitcast.1) | data formatting | bytes 16384

commit v4 on v3

--- a/solution.py
+++ b/solution.py
@@ -152,22 +152,27 @@
     def send_greens(dx, dz):
         piece = greens_here.at[OUTGOING.index((dx, dz))]
         greens_in[dx, dz].wait()
-        if dx == 0:
-            send(piece, own.at[:, rows(mine), :], g_send, g_recv.at[mine], (0, 0, dz))
-        elif dz == 1:
-            send(piece, stage_z.at[dx - 1], g_send, stage_recv.at[0, dx - 1], (0, 0, dz))
-        else:
-            send(piece, stage_x.at[dx - 1], g_send, stage_recv.at[1, dx - 1], (dx, 0, 0))
+        for c in range(2):
+            if dx == 0:
+                send(piece.at[c], own.at[c, rows(mine), :], g_send, g_recv.at[mine, c], (0, 0, dz))
+            elif dz == 1:
+                send(piece.at[c], stage_z.at[dx - 1, c], g_send, stage_recv.at[0, dx - 1, c], (0, 0, dz))
+            else:
+                send(piece.at[c], stage_x.at[dx - 1, c], g_send, stage_recv.at[1, dx - 1, c], (dx, 0, 0))
 
     def forward_x(dx):
-        piece, index = stage_z.at[dx - 1], rank(0, 3)
-        arrived(piece, stage_recv.at[0, dx - 1])
-        send(piece, own.at[:, rows(index), :], forward_send, g_recv.at[index], (dx, 0, 0))
+        index = rank(0, 3)
+        for c in range(2):
+            piece = stage_z.at[dx - 1, c]
+            arrived(piece, stage_recv.at[0, dx - 1, c])
+            send(piece, own.at[c, rows(index), :], forward_send, g_recv.at[index, c], (dx, 0, 0))
 
     def forward_z(dx):
-        piece, index = stage_x.at[dx - 1], rank(-dx, 0)
-        arrived(piece, stage_recv.at[1, dx - 1])
-        send(piece, own.at[:, rows(index), :], forward_send, g_recv.at[index], (0, 0, 3))
+        index = rank(-dx, 0)
+        for c in range(2):
+            piece = stage_x.at[dx - 1, c]
+            arrived(piece, stage_recv.at[1, dx - 1, c])
+            send(piece, own.at[c, rows(index), :], forward_send, g_recv.at[index, c], (0, 0, 3))
 
     def send_weights(dz, d):
         kept = (z + dz) % SIDE // 2
@@ -175,74 +180,76 @@
 
         @brings
         def to_neighbour():
-            send(
-                weights_here.at[:, kept, d, :, columns],
-                stage_w.at[-dz % SIDE // 2] if d == 2 else mix.at[:, d, rows(mine), columns],
-                wz_send,
-                wz_recv.at[-dz % SIDE // 2, d],
-                (0, 0, dz),
-            )
+            for c in range(2):
+                send(
+                    weights_here.at[c, kept, d, :, columns],
+                    stage_w.at[-dz % SIDE // 2, c] if d == 2 else mix.at[c, d, rows(mine), columns],
+                    wz_send,
+                    wz_recv.at[-dz % SIDE // 2, d, c],
+                    (0, 0, dz),
+                )
 
     def columns_of(d, dz, zs):
         return at_multiple(zs, HALF, HALF) if d == 0 and dz == 3 else slice(None)
 
-    def mix_at(index, d, dz):
-        return mix.at[:, d, rows(index), columns_of(d, dz, (z + dz) % SIDE // 2)]
-
-    def to_twin(index, d, dz):
-        piece = mix_at(index, d, dz)
+    def mix_at(index, d, dz, c):
+        return mix.at[c, d, rows(index), columns_of(d, dz, (z + dz) % SIDE // 2)]
+
+    def to_twin(piece, d, dz):
         send(piece, piece, wt_send.at[d], wt_recv.at[dz // 2, d], (0, 0, 0, 1))
 
     def green_piece(dx, dz):
         index = rank(dx, dz)
-        piece = own.at[:, rows(index), :]
-        arrived(piece, g_recv.at[index])
-        send(piece, near.at[:, rows(index), :], near_send, near_recv.at[dz // 2], (0, 3, 0))
         other = at_multiple((y + 1) % SIDE // 2, HALF, HALF)
-        send(own.at[:, rows(index), other], far.at[:, rows(index), :], far_send, far_recv, (0, 1, 0))
-
-    def spread_weights(index, d, dz):
-        piece = mix_at(index, d, dz)
+        for c in range(2):
+            piece = own.at[c, rows(index), :]
+            arrived(piece, g_recv.at[index, c])
+            send(piece, near.at[c, rows(index), :], near_send, near_recv.at[dz // 2], (0, 3, 0))
+            send(own.at[c, rows(index), other], far.at[c, rows(index), :], far_send, far_recv, (0, 1, 0))
+
+    def spread_weights(piece, d, dz, c):
         for dx in (1, 3):
-            send(piece, piece, wx_send, wx_recv.at[SIDE - dx - 1, dz // 2, d], (dx, 0, 0))
-        to_twin(index, d, dz)
+            send(piece, piece, wx_send, wx_recv.at[SIDE - dx - 1, dz // 2, d, c], (dx, 0, 0))
+        to_twin(piece, d, dz)
 
     def weights_along_z(d, dz):
         @brings
         def onward():
-            index = rank(0, dz)
-            if d == 2:
-                piece = stage_w.at[dz // 2]
-                arrived(piece, wz_recv.at[dz // 2, d])
-                send(piece, mix_at(index, d, dz), wy_send, wy_recv.at[dz // 2], (0, 1, 0))
-            else:
-                arrived(mix_at(index, d, dz), wz_recv.at[dz // 2, d])
-                spread_weights(index, d, dz)
+            for c in range(2):
+                piece = mix_at(rank(0, dz), d, dz, c)
+                if d == 2:
+                    arrived(stage_w.at[dz // 2, c], wz_recv.at[dz // 2, d, c])
+                    send(stage_w.at[dz // 2, c], piece, wy_send, wy_recv.at[dz // 2, c], (0, 1, 0))
+                else:
+                    arrived(piece, wz_recv.at[dz // 2, d, c])
+                    spread_weights(piece, d, dz, c)
 
     def weights_along_y(dz):
         @brings
         def onward():
-            index = rank(0, dz)
-            arrived(mix_at(index, 2, dz), wy_recv.at[dz // 2])
-            spread_weights(index, 2, dz)
+            for c in range(2):
+                piece = mix_at(rank(0, dz), 2, dz, c)
+                arrived(piece, wy_recv.at[dz // 2, c])
+                spread_weights(piece, 2, dz, c)
 
     def weights_along_x(d, dz):
         @brings
-        def spread_out():
-            for k, dx in enumerate((1, 3)):
-                index = rank(dx, dz)
-                piece = mix_at(index, d, dz)
-                arrived(piece, wx_recv.at[dx - 1, dz // 2, d])
-                if dz // 2 == k:
-                    send(piece, piece, wx_send, wx_recv.at[1, dz // 2, d], (-dx % SIDE, 0, 0))
-                to_twin(index, d, dz)
+        def onward():
+            for c in range(2):
+                for k, dx in enumerate((1, 3)):
+                    piece = mix_at(rank(dx, dz), d, dz, c)
+                    arrived(piece, wx_recv.at[dx - 1, dz // 2, d, c])
+                    if dz // 2 == k:
+                        send(piece, piece, wx_send, wx_recv.at[1, dz // 2, d, c], (-dx % SIDE, 0, 0))
+                    to_twin(piece, d, dz)
 
     def weights_across(d, dz):
         @brings
         def hand_over():
-            index = rank(2, dz)
-            arrived(mix_at(index, d, dz), wx_recv.at[1, dz // 2, d])
-            to_twin(index, d, dz)
+            for c in range(2):
+                piece = mix_at(rank(2, dz), d, dz, c)
+                arrived(piece, wx_recv.at[1, dz // 2, d, c])
+                to_twin(piece, d, dz)
 
     def weights_from_twin(d, dz):
         @pl.when(core == 0)
@@ -418,17 +425,17 @@
             pltpu.VMEM((8, POINTS), jnp.float32),
             pltpu.VMEM((ranks, 1, POINTS), jnp.float32),
             dma,
-            dma((ranks,)),
+            dma((ranks, 2)),
             dma,
             dma((2,)),
             dma,
-            dma((2,)),
-            dma,
-            dma,
-            dma,
-            dma((2, 3)),
-            dma,
-            dma((3, 2, 3)),
+            dma((2, 2)),
+            dma,
+            dma,
+            dma,
+            dma((2, 3, 2)),
+            dma,
+            dma((3, 2, 3, 2)),
             dma((3,)),
             dma((2, 3)),
             dma,
@@ -440,7 +447,7 @@
             dma((spread + 1,)),
             pltpu.VMEM((3, 2, RUN, POINTS), jnp.bfloat16),
             pltpu.VMEM((3, 2, RUN, POINTS), jnp.bfloat16),
-            dma((2, 3)),
+            dma((2, 3, 2)),
             dma,
             pltpu.SemaphoreType.REGULAR,
         ],

time: 50.5 us -> 49.9 us (0.988)
  Pallas kernels: 49.8 us -> 49.2 us
    pallas_call x1, Pallas kernels: 49.8 us -> 49.2 us  [body(): pl.pallas_call(kernel, out_shape=jax.ShapeDtypeStruct((SIDE, 1, POINTS),...]
where the time goes in v4:
time: 49.9 us; the launch traced here: 49.8 us
  Pallas kernels  49.2 us (99%)
  local copies, waits for them, and re-layouts  0.6 us (1%)
    pallas_call x1, Pallas kernels, body(): pl.pallas_call(kernel, out_shape=jax.ShapeDtypeStruct((SIDE, 1, POINTS),...  49.2 us

profile of v4, /device:TPU:1, one launch (start us, length us, event | category | flops | bytes accessed | tf_op | source)
XLA Modules:
  0.0 49.8 jit_solution(15521890455058477440)
XLA Ops:
  0.0 49.2 %shard_map.28 = f32[4,1,512]{2,1,0:T(1,128)S(1)} custom-call(bf16[2,2,64,2048]{3,2,1,0:T(8,128)(2,1)} %greens.1, bf16[2,2,64,2048]{3,2,1,0:T(8,128)(2,1)} %weights.1), custom_call_target="tpu_custom_call" | custom-call | tf_op jit(solution)/shard_map/pallas_call | solution.py:413
  49.2 0.6 %copy.4 = f32[2048]{0:T(1024)} copy(f32[2048]{0:T(1024)S(1)} %bitcast.1) | data formatting | bytes 16384

commit v5 on v4

--- a/solution.py
+++ b/solution.py
@@ -324,31 +324,31 @@
     weights_along_z(0, 1)
     forward_x(1)
     weights_along_z(2, 1)
+    forward_x(3)
+    forward_z(2)
     weights_along_z(1, 1)
-    forward_z(2)
-    forward_x(3)
+    weights_along_x(0, 1)
     green_piece(3, 1)
-    weights_along_x(0, 1)
     weights_along_y(1)
     weights_along_z(0, 3)
     green_piece(3, 3)
     weights_along_z(2, 3)
     weights_along_x(1, 1)
+    green_piece(1, 1)
     weights_across(0, 1)
     weights_along_z(1, 3)
-    green_piece(1, 1)
     weights_along_x(2, 1)
+    green_piece(1, 3)
     forward_x(2)
-    green_piece(1, 3)
+    weights_along_x(0, 3)
     weights_along_y(3)
-    weights_along_x(0, 3)
     weights_across(1, 1)
     green_piece(2, 1)
     weights_across(2, 1)
     weights_along_x(1, 3)
-    weights_across(0, 3)
     pl.semaphore_wait(met, 1)
     green_piece(2, 3)
+    weights_across(0, 3)
     weights_along_x(2, 3)
     weights_across(1, 3)
     add_own(1)

time: 49.9 us -> 50.4 us (1.010)
    pallas_call x1, Pallas kernels: 49.2 us -> 49.7 us  [body(): pl.pallas_call(kernel, out_shape=jax.ShapeDtypeStruct((SIDE, 1, POINTS),...]
where the time goes in v5:
time: 50.4 us; the launch traced here: 50.3 us
  Pallas kernels  49.7 us (99%)
  local copies, waits for them, and re-layouts  0.6 us (1%)
    pallas_call x1, Pallas kernels, body(): pl.pallas_call(kernel, out_shape=jax.ShapeDtypeStruct((SIDE, 1, POINTS),...  49.7 us

profile of v5, /device:TPU:1, one launch (start us, length us, event | category | flops | bytes accessed | tf_op | source)
XLA Modules:
  0.0 50.3 jit_solution(18148847102903658123)
XLA Ops:
  0.0 49.7 %shard_map.28 = f32[4,1,512]{2,1,0:T(1,128)S(1)} custom-call(bf16[2,2,64,2048]{3,2,1,0:T(8,128)(2,1)} %greens.1, bf16[2,2,64,2048]{3,2,1,0:T(8,128)(2,1)} %weights.1), custom_call_target="tpu_custom_call" | custom-call | tf_op jit(solution)/shard_map/pallas_call | solution.py:413
  49.7 0.6 %copy.4 = f32[2048]{0:T(1024)} copy(f32[2048]{0:T(1024)S(1)} %bitcast.1) | data formatting | bytes 16384
